TPU v7x, 32 devices: a whole 2x2x4 slice. The times are simulated.
32 devices in a mesh: wide: 8 (over y, x, core), narrow: 4 (over z).
Axes of the slice: x: 2, y: 2, z: 4, core: 2. Of those that a mesh axis runs over, the one named last changes fastest.
Arguments:
- momentum: float32 [9216, 9216], P('wide', 'narrow'), may hold values from -3 to 3
- gradient: bfloat16 [9216, 9216], P('wide', 'narrow'), may hold values from -48 to 48
- right_factor: float32 [512, 9216], P('wide', 'narrow'), may hold values from -6 to 6
Outputs:
- new_momentum: float32 [9216, 9216], P('wide', 'narrow')
- new_right: float32 [512, 9216], P('wide', 'narrow')
- update: bfloat16 [9216, 9216], P('wide', 'narrow')
All inputs are finite; a program needn't handle non-finite values.
Results may differ from a plain program's by a relative error of at most 0.001.
Values sent between devices are 32-bit elements; how exact they have to be, the bound alone decides.
No kernel may reach another device: no remote copies, remote signals or barrier semaphores. Data moves between devices by JAX's collectives and lax.ppermute only.
A program may use at most 128 MiB of HBM per device.

v0:
```python
import jax
import jax.numpy as jnp
from jax import lax
from jax.sharding import PartitionSpec as P

N_COLS = 9216
EPS = 1e-06
MU = 0.95


def orthonormal(projected, gram_matrix):
    factor_lower = jnp.linalg.cholesky(gram_matrix)
    return jax.scipy.linalg.solve_triangular(factor_lower, projected.T, lower=True).T


def matmul(left, right):
    return jnp.dot(left, right, preferred_element_type=jnp.float32, precision=lax.Precision.HIGHEST)


def per_device(momentum, gradient, right_factor):
    blended = momentum + gradient.astype(jnp.float32)
    partial_left = matmul(blended, lax.all_gather(right_factor, "wide", axis=0, tiled=True).T)
    projected = lax.psum(partial_left, "narrow")
    gram_matrix = lax.psum(matmul(projected.T, projected), "wide")
    left_basis = orthonormal(projected, gram_matrix)
    columns = left_basis
    right_block = lax.psum_scatter(
        matmul(columns.T, blended), "wide", scatter_dimension=0, tiled=True
    )
    squares = lax.psum(jnp.sum(right_block * right_block, axis=1), "narrow")
    root_mean = jnp.sqrt(squares / N_COLS + EPS)
    new_right = right_block / root_mean[:, None]
    pieces = (
        lax.all_gather(right_block, "wide", axis=0, tiled=True),
        lax.all_gather(root_mean, "wide", axis=0, tiled=True),
    )
    columns = left_basis
    normed = pieces[0] / pieces[1][:, None]
    feedback = matmul(columns, pieces[0])
    direction = matmul(columns, normed)
    new_momentum = blended - (1.0 - MU) * feedback
    return (new_momentum, new_right, direction.astype(jnp.bfloat16))


def solution(mesh):
    return jax.shard_map(
        per_device,
        mesh=mesh,
        in_specs=(P("wide", "narrow"), P("wide", "narrow"), P("wide", "narrow")),
        out_specs=(P("wide", "narrow"), P("wide", "narrow"), P("wide", "narrow")),
        check_vma=False,
    )
```

profile of v0, /device:TPU:0, one launch (start us, length us, event | category | flops | bytes accessed | tf_op | source)
XLA Modules:
  0.0 566.0 jit_solution(15770033689719844626)
XLA Ops:
  7.9 43.5 %all-gather.3.cloned.1.call-done = f32[512,2304]{1,0:T(8,128)} async-done(((f32[64,2304]{1,0:T(8,128)}), f32[512,2304]{1,0:T(8,128)}) %all-gather.3.cloned.1.call-update) | async-done | bytes 4718608 | tf_op jit(solution)/shard_map/all_gather | solution.py:22
  51.4 22.9 %fusion.3 = f32[1152,512]{1,0:T(8,128)} fusion(f32[512,2304]{1,0:T(8,128)} %all-gather.3.cloned.1.call-done, f32[1152,2304]{1,0:T(8,128)} %param.3, bf16[1152,2304]{1,0:T(8,128)(2,1)} %param.4), kind=kOutput, calls=%fused_computation.8 | convolution fusion | flops 16312762368 | bytes 23003136 | tf_op jit(solution)/shard_map/dot_general | solution.py:17
  74.4 94.7 %all-reduce.5.cloned.1.call-done = f32[1152,512]{1,0:T(8,128)} async-done(((f32[1152,512]{1,0:T(8,128)}), f32[1152,512]{1,0:T(8,128)}) %all-reduce.5.cloned.1.call-update) | async-done | bytes 2359312 | tf_op jit(solution)/shard_map/psum | solution.py:23
  169.1 7.7 %fusion.40 = f32[512,512]{0,1:T(8,128)} fusion(f32[1152,512]{1,0:T(8,128)} %all-reduce.5.cloned.1.call-done), kind=kOutput, calls=%fused_computation.82 | convolution fusion | flops 3623878656 | bytes 3407872 | tf_op jit(solution)/shard_map/dot_general | solution.py:17
  177.1 55.6 %all-reduce.7.cloned.1.call-done = f32[512,512]{0,1:T(8,128)} async-done(((f32[512,512]{0,1:T(8,128)}), f32[512,512]{0,1:T(8,128)}) %all-reduce.7.cloned.1.call-update) | async-done | bytes 1048592 | tf_op jit(solution)/shard_map/psum | solution.py:24
  235.6 11.7 %cholesky.104 = f32[128,128]{1,0:T(8,128)S(1)} custom-call(f32[128,128]{1,0:T(8,128)S(1)} %cholesky.266), custom_call_target="Cholesky" | custom-call | tf_op jit(solution)/shard_map/jit(cholesky)/cholesky | solution.py:12
  247.3 9.8 %custom-call.31 = f32[1,128,128]{1,2,0:T(8,128)S(1)} custom-call(f32[1,128,128]{2,1,0:T(8,128)S(1)} %get-tuple-element.30), custom_call_target="InvertDiagBlocksLowerTriangular" | custom-call | tf_op jit(solution)/shard_map/jit(cholesky)/cholesky | solution.py:12
  259.8 11.7 %cholesky.217 = f32[128,128]{1,0:T(8,128)S(1)} custom-call(f32[128,128]{1,0:T(8,128)S(1)} %cholesky.270), custom_call_target="Cholesky" | custom-call | tf_op jit(solution)/shard_map/jit(cholesky)/cholesky | solution.py:12
  271.5 10.2 %custom-call.32 = f32[1,128,128]{1,2,0:T(8,128)S(1)} custom-call(f32[1,128,128]{2,1,0:T(8,128)S(1)} %get-tuple-element.27), custom_call_target="InvertDiagBlocksLowerTriangular" | custom-call | tf_op jit(solution)/shard_map/jit(cholesky)/cholesky | solution.py:12
  284.1 13.2 %cholesky.238 = f32[128,128]{1,0:T(8,128)} custom-call(f32[128,128]{1,0:T(8,128)} %cholesky.275), custom_call_target="Cholesky" | custom-call | tf_op jit(solution)/shard_map/jit(cholesky)/cholesky | solution.py:12
  299.4 11.3 %custom-call.33 = f32[1,128,128]{1,2,0:T(8,128)} custom-call(f32[1,128,128]{2,1,0:T(8,128)} %get-tuple-element.24), custom_call_target="InvertDiagBlocksLowerTriangular" | custom-call | tf_op jit(solution)/shard_map/jit(cholesky)/cholesky | solution.py:12
  313.0 11.7 %cholesky.255 = f32[128,128]{1,0:T(8,128)S(1)} custom-call(f32[128,128]{1,0:T(8,128)S(1)} %convolution_subtract_fusion.5), custom_call_target="Cholesky" | custom-call | tf_op jit(solution)/shard_map/jit(cholesky)/cholesky | solution.py:12
  329.8 13.7 %while.1 = (s32[]{:T(128)}, f32[512,512]{1,0:T(8,128)}, s32[4,2]{0,1:T(2,128)S(1)}, f32[4,128,128]{2,1,0:T(8,128)}, s32[]{:T(128)}) while((s32[]{:T(128)}, f32[512,512]{1,0:T(8,128)}, s32[4,2]{0,1:T(2,128)S(1)}, f32[4,128,128]{2,1,0:T(8,128)}, s32[]{:T(128)}) %tuple.32), condition=%wide.while_cond, body=%wide.while_body.sunk | while | flops 2 | bytes 132205 | solution.py:13
  333.8 2.8 bitcast_dynamic-update-slice_fusion.2
  343.5 40.1 %custom-call.34 = f32[4,128,128]{1,2,0:T(8,128)S(1)} custom-call(f32[4,128,128]{2,1,0:T(8,128)} %get-tuple-element.10), custom_call_target="InvertDiagBlocksLowerTriangular" | custom-call | tf_op jit(solution)/shard_map/jit(_solve_triangular)/triangular_solve | solution.py:13
  388.4 3.0 convolution_subtract_fusion.1
  392.2 4.2 convolution_subtract_fusion
  397.3 23.1 %fusion.2 = f32[512,2304]{1,0:T(8,128)} fusion(f32[1152,2304]{1,0:T(8,128)} %param.3, bf16[1152,2304]{1,0:T(8,128)(2,1)S(1)} %bitcast.55, f32[128,1152]{1,0:T(8,128)S(1)} %fusion.24, f32[128,1152]{1,0:T(8,128)S(1)} %fusion.25, f32[128,1152]{1,0:T(8,128)S(1)} %fusion.27, f32[128,1152]{1,0:T(8,128)S(1)} %fusion.14), kind=kOutput, calls=%fused_computation.7 | convolution fusion | flops 16314531840 | bytes 23003136 | tf_op jit(solution)/shard_map/dot_general | solution.py:17
  420.4 53.1 %reduce-scatter.2.cloned.1.call-done = f32[64,2304]{1,0:T(8,128)} async-done(((f32[512,2304]{1,0:T(8,128)}), f32[64,2304]{1,0:T(8,128)}) %reduce-scatter.2.cloned.1.call-update) | async-done | bytes 589840 | tf_op jit(solution)/shard_map/reduce_scatter | solution.py:27
  476.0 11.7 %psum.23 = f32[64]{0:T(128)S(1)} all-reduce(f32[64]{0:T(128)S(1)} %multiply_reduce_fusion), channel_id=1, replica_groups=mesh['wide'=8,'narrow'=4] {'narrow'}, use_global_device_ids=true, to_apply=%region_12.13 | all-reduce | flops 64 | bytes 512 | tf_op jit(solution)/shard_map/psum | solution.py:30
  487.8 12.1 %all-reduce.1 = f32[512]{0:T(512)S(1)} all-reduce(f32[512]{0:T(512)S(1)} %get-tuple-element.31), channel_id=1, replica_groups=mesh['wide'=8,'narrow'=4] {'wide'}, use_global_device_ids=true, to_apply=%add.1 | all-reduce | flops 512 | bytes 4096
  501.9 12.3 %all-gather.5.cloned.1.call-done = f32[512,2304]{1,0:T(8,128)} async-done(((f32[64,2304]{1,0:T(8,128)}), f32[512,2304]{1,0:T(8,128)}) %all-gather.5.cloned.1.call-update) | async-done | bytes 4718608 | tf_op jit(solution)/shard_map/all_gather | solution.py:34
  514.2 24.1 %fusion = f32[1152,2304]{1,0:T(8,128)} fusion(f32[512,2304]{1,0:T(8,128)} %all-gather.5.cloned.1.call-done, f32[1152,2304]{1,0:T(8,128)} %param.3, bf16[1152,2304]{1,0:T(8,128)(2,1)} %param.4, f32[128,1152]{1,0:T(8,128)S(1)} %fusion.24, f32[128,1152]{1,0:T(8,128)S(1)} %copy-done.2, f32[128,1152]{1,0:T(8,128)S(1)} %fusion.27, f32[128,1152]{1,0:T(8,128)S(1)} %fusion.14), kind=kOutput, calls=%fused_computation.3 | convolution fusion | flops 16319840256 | bytes 33619968 | tf_op jit(solution)/shard_map/dot_general | solution.py:17
  538.3 20.7 %convolution_convert_fusion = bf16[1152,2304]{1,0:T(8,128)(2,1)} fusion(f32[512,2304]{1,0:T(8,128)S(1)} %copy-done.3, f32[512]{0:T(512)S(1)} %all-reduce.1, f32[128,1152]{1,0:T(8,128)S(1)} %fusion.24, f32[128,1152]{1,0:T(8,128)S(1)} %copy-done.2, f32[128,1152]{1,0:T(8,128)S(1)} %fusion.27, f32[128,1152]{1,0:T(8,128)S(1)} %fusion.14), kind=kOutput, calls=%fused_computation.4 | convolution fusion | flops 16313057280 | bytes 12388352 | tf_op jit(solution)/shard_map/dot_general | solution.py:17
  (77 shorter events, 37.0 us)
Async XLA Ops:
  7.2 44.2 %all-gather.3.cloned.1.call-start = ((), (), s32[]{:S(2)}) async-start(), calls=%async_computation.1 | async-start | bytes 5308416 | tf_op jit(solution)/shard_map/all_gather | solution.py:22
  7.9 161.2 %all-reduce.5.cloned.1.call-start = ((), (), s32[]{:S(2)}) async-start(), calls=%async_computation.2 | async-start | bytes 4718592 | tf_op jit(solution)/shard_map/psum | solution.py:23
  74.3 158.4 %all-reduce.7.cloned.1.call-start = ((), (), s32[]{:S(2)}) async-start(), calls=%async_computation.3 | async-start | bytes 2097152 | tf_op jit(solution)/shard_map/psum | solution.py:24
  176.8 296.7 %reduce-scatter.2.cloned.1.call-start = ((), (), s32[]{:S(2)}) async-start(), calls=%async_computation.4 | async-start | bytes 5308416 | tf_op jit(solution)/shard_map/reduce_scatter | solution.py:27
  232.7 1.7 copy-start.4
  234.6 1.0 copy-start.5
  282.0 101.6 %copy-start = (f32[1152,512]{1,0:T(8,128)S(1)}, f32[1152,512]{1,0:T(8,128)}, u32[]{:S(2)}) copy-start(f32[1152,512]{1,0:T(8,128)} %all-reduce.5.cloned.1.call-done) | copy-start | bytes 7077892
  383.6 0.8 copy-start.6
  383.6 13.6 %slice-start = ((s8[5308416]{0:T(1024)(128)(4,1)}), s8[4194304]{0:T(1024)(128)(4,1)S(1)}, s32[]{:S(2)}) async-start(s8[5308416]{0:T(1024)(128)(4,1)} %bitcast.54), calls=%async_computation.6 | async-start | bytes 8388608
  386.8 4.7 copy-start.7
  388.4 8.8 %slice-start.1 = ((s8[5308416]{0:T(1024)(128)(4,1)}), s8[1114112]{0:T(1024)(128)(4,1)S(1)}, s32[]{:S(2)}) async-start(s8[5308416]{0:T(1024)(128)(4,1)} %bitcast.54), calls=%async_computation.7 | async-start | bytes 2228224
  392.2 5.0 copy-start.1
  420.3 53.2 %copy-start.8 = (u32[32]{0:T(128)S(1)}, u32[32]{0:T(128)}, u32[]{:S(2)}) copy-start(u32[32]{0:T(128)} %constant.172) | copy-start | bytes 388
  420.4 93.8 %copy-start.2 = (f32[128,1152]{1,0:T(8,128)S(1)}, f32[128,1152]{1,0:T(8,128)}, u32[]{:S(2)}) copy-start(f32[128,1152]{1,0:T(8,128)} %copy-done.1) | copy-start | bytes 1769476
  420.4 93.8 %all-gather.5.cloned.1.call-start = ((), (), s32[]{:S(2)}) async-start(), calls=%async_computation.5 | async-start | bytes 5308416 | tf_op jit(solution)/shard_map/all_gather | solution.py:34
  514.2 24.1 %copy-start.3 = (f32[512,2304]{1,0:T(8,128)S(1)}, f32[512,2304]{1,0:T(8,128)}, u32[]{:S(2)}) copy-start(f32[512,2304]{1,0:T(8,128)} %all-gather.5.cloned.1.call-done) | copy-start | bytes 14155780
Sparse Core Ops, SparseCore 0:
  9.9 41.4 all-gather.2
  74.4 94.6 all-reduce.4
  176.9 55.7 all-reduce.6
  420.5 53.0 reduce-scatter.1
  475.3 38.9 all-gather.4
where the time goes:
time: 574 us; the launch traced here: 566 us
  waiting for transfers between devices  260 us (45%)
  other arithmetic  128 us (22%)
  matrix products  118 us (21%)
  blocking collectives  23.8 us (4%)
  between operations  17.8 us (3%)
  local copies, waits for them, and re-layouts  17.7 us (3%)
    dot_general x5, matrix products, matmul(): jnp.dot(left, right, preferred_element_type=jnp.float32, precision=lax.Pr...  98.4 us
    psum x1, waiting for transfers between devices, per_device(): projected = lax.psum(partial_left, 'narrow')  94.7 us
    another operation x14, other arithmetic, orthonormal(): factor_lower = jnp.linalg.cholesky(gram_matrix)  83.1 us
    psum x1, waiting for transfers between devices, per_device(): gram_matrix = lax.psum(matmul(projected.T, projected), 'wide')  55.6 us
    reduce_scatter x1, waiting for transfers between devices, per_device(): lax.psum_scatter(matmul(columns.T, blended), 'wide', scatter_dimension=0,...  53.1 us
    all_gather x1, waiting for transfers between devices, per_device(): lax.all_gather(right_factor, 'wide', axis=0, tiled=True)  43.5 us
    another operation x3, other arithmetic, orthonormal(): jax.scipy.linalg.solve_triangular(factor_lower, projected.T, lower=True)  41.4 us
    another operation x12, local copies, waits for them, and re-layouts  13.7 us
  transfers between devices with their start and end apart: 5, of which 5 were waited for; matrix products, arithmetic and copies ran while one was open for 1% of the time, Pallas kernels for 0%

commit v1 on v0

--- a/solution.py
+++ b/solution.py
@@ -20,7 +20,7 @@
 def per_device(momentum, gradient, right_factor):
     blended = momentum + gradient.astype(jnp.float32)
     partial_left = matmul(blended, lax.all_gather(right_factor, "wide", axis=0, tiled=True).T)
-    projected = lax.psum(partial_left, "narrow")
+    projected = jnp.sum(lax.all_gather(partial_left, "narrow"), axis=0)
     gram_matrix = lax.psum(matmul(projected.T, projected), "wide")
     left_basis = orthonormal(projected, gram_matrix)
     columns = left_basis

time: 574 us -> 654 us (1.14)
  waiting for transfers between devices: 260 us -> 331 us
    all_gather x0 -> x1, waiting for transfers between devices: none -> 167 us  [per_device(): projected = jnp.sum(lax.all_gather(partial_left, 'narrow'), axis=0)]
    psum x1 -> x0, waiting for transfers between devices: 94.7 us -> none  [per_device(): projected = lax.psum(partial_left, 'narrow')]
where the time goes in v1:
time: 654 us; the launch traced here: 645 us
  waiting for transfers between devices  331 us (51%)
  other arithmetic  134 us (20%)
  matrix products  117 us (18%)
  blocking collectives  23.8 us (4%)
  local copies, waits for them, and re-layouts  20.1 us (3%)
  between operations  17.8 us (3%)
    all_gather x1, waiting for transfers between devices, per_device(): projected = jnp.sum(lax.all_gather(partial_left, 'narrow'), axis=0)  167 us
    dot_general x5, matrix products, matmul(): jnp.dot(left, right, preferred_element_type=jnp.float32, precision=lax.Pr...  96 us
    another operation x14, other arithmetic, orthonormal(): factor_lower = jnp.linalg.cholesky(gram_matrix)  83.2 us
    psum x1, waiting for transfers between devices, per_device(): gram_matrix = lax.psum(matmul(projected.T, projected), 'wide')  54.8 us
    reduce_scatter x1, waiting for transfers between devices, per_device(): lax.psum_scatter(matmul(columns.T, blended), 'wide', scatter_dimension=0,...  53.1 us
    all_gather x1, waiting for transfers between devices, per_device(): lax.all_gather(right_factor, 'wide', axis=0, tiled=True)  43.5 us
    another operation x3, other arithmetic, orthonormal(): jax.scipy.linalg.solve_triangular(factor_lower, projected.T, lower=True)  41.4 us
    another operation x12, local copies, waits for them, and re-layouts  14.5 us
  transfers between devices with their start and end apart: 5, of which 5 were waited for; matrix products, arithmetic and copies ran while one was open for 1% of the time, Pallas kernels for 0%

profile of v1, /device:TPU:0, one launch (start us, length us, event | category | flops | bytes accessed | tf_op | source)
XLA Modules:
  0.0 644.6 jit_solution(4743406619204210991)
XLA Ops:
  7.9 43.5 %all-gather.5.cloned.1.call-done = f32[512,2304]{1,0:T(8,128)} async-done(((f32[64,2304]{1,0:T(8,128)}), f32[512,2304]{1,0:T(8,128)}) %all-gather.5.cloned.1.call-update) | async-done | bytes 4718608 | tf_op jit(solution)/shard_map/all_gather | solution.py:22
  51.4 22.9 %fusion.3 = f32[1152,512]{1,0:T(8,128)} fusion(f32[512,2304]{1,0:T(8,128)} %all-gather.5.cloned.1.call-done, f32[1152,2304]{1,0:T(8,128)} %param.3, bf16[1152,2304]{1,0:T(8,128)(2,1)} %param.4), kind=kOutput, calls=%fused_computation.8 | convolution fusion | flops 16312762368 | bytes 23003136 | tf_op jit(solution)/shard_map/dot_general | solution.py:17
  74.4 166.9 %all-gather.9.cloned.1.call-done = f32[4608,512]{1,0:T(8,128)} async-done(((f32[1152,512]{1,0:T(8,128)}), f32[4608,512]{1,0:T(8,128)}) %all-gather.9.cloned.1.call-update) | async-done | bytes 9437200 | tf_op jit(solution)/shard_map/all_gather | solution.py:23
  241.2 5.1 reduce_sum.18
  246.3 5.3 fusion.40
  252.0 54.8 %all-reduce.4.cloned.1.call-done = f32[512,512]{0,1:T(8,128)} async-done(((f32[512,512]{0,1:T(8,128)}), f32[512,512]{0,1:T(8,128)}) %all-reduce.4.cloned.1.call-update) | async-done | bytes 1048592 | tf_op jit(solution)/shard_map/psum | solution.py:24
  311.8 11.7 %cholesky.104 = f32[128,128]{1,0:T(8,128)S(1)} custom-call(f32[128,128]{1,0:T(8,128)S(1)} %cholesky.266), custom_call_target="Cholesky" | custom-call | tf_op jit(solution)/shard_map/jit(cholesky)/cholesky | solution.py:12
  323.7 9.8 %custom-call.31 = f32[1,128,128]{1,2,0:T(8,128)S(1)} custom-call(f32[1,128,128]{2,1,0:T(8,128)S(1)} %get-tuple-element.30), custom_call_target="InvertDiagBlocksLowerTriangular" | custom-call | tf_op jit(solution)/shard_map/jit(cholesky)/cholesky | solution.py:12
  336.7 11.7 %cholesky.217 = f32[128,128]{1,0:T(8,128)S(1)} custom-call(f32[128,128]{1,0:T(8,128)S(1)} %cholesky.270), custom_call_target="Cholesky" | custom-call | tf_op jit(solution)/shard_map/jit(cholesky)/cholesky | solution.py:12
  348.4 10.2 %custom-call.32 = f32[1,128,128]{1,2,0:T(8,128)S(1)} custom-call(f32[1,128,128]{2,1,0:T(8,128)S(1)} %get-tuple-element.27), custom_call_target="InvertDiagBlocksLowerTriangular" | custom-call | tf_op jit(solution)/shard_map/jit(cholesky)/cholesky | solution.py:12
  361.7 13.2 %cholesky.238 = f32[128,128]{1,0:T(8,128)} custom-call(f32[128,128]{1,0:T(8,128)} %cholesky.275), custom_call_target="Cholesky" | custom-call | tf_op jit(solution)/shard_map/jit(cholesky)/cholesky | solution.py:12
  377.0 11.3 %custom-call.33 = f32[1,128,128]{1,2,0:T(8,128)} custom-call(f32[1,128,128]{2,1,0:T(8,128)} %get-tuple-element.24), custom_call_target="InvertDiagBlocksLowerTriangular" | custom-call | tf_op jit(solution)/shard_map/jit(cholesky)/cholesky | solution.py:12
  390.6 11.7 %cholesky.255 = f32[128,128]{1,0:T(8,128)S(1)} custom-call(f32[128,128]{1,0:T(8,128)S(1)} %convolution_subtract_fusion.5), custom_call_target="Cholesky" | custom-call | tf_op jit(solution)/shard_map/jit(cholesky)/cholesky | solution.py:12
  407.6 14.5 %while.1 = (s32[]{:T(128)}, f32[512,512]{1,0:T(8,128)}, s32[4,2]{0,1:T(2,128)S(1)}, f32[4,128,128]{2,1,0:T(8,128)}, s32[]{:T(128)}) while((s32[]{:T(128)}, f32[512,512]{1,0:T(8,128)}, s32[4,2]{0,1:T(2,128)S(1)}, f32[4,128,128]{2,1,0:T(8,128)}, s32[]{:T(128)}) %tuple.32), condition=%wide.while_cond, body=%wide.while_body.sunk | while | flops 2 | bytes 132205 | solution.py:13
  422.1 40.1 %custom-call.34 = f32[4,128,128]{1,2,0:T(8,128)S(1)} custom-call(f32[4,128,128]{2,1,0:T(8,128)} %get-tuple-element.10), custom_call_target="InvertDiagBlocksLowerTriangular" | custom-call | tf_op jit(solution)/shard_map/jit(_solve_triangular)/triangular_solve | solution.py:13
  467.0 3.0 convolution_subtract_fusion.1
  470.8 4.2 convolution_subtract_fusion
  475.9 23.1 %fusion.2 = f32[512,2304]{1,0:T(8,128)} fusion(f32[1152,2304]{1,0:T(8,128)} %param.3, bf16[1152,2304]{1,0:T(8,128)(2,1)S(1)} %bitcast.60, f32[128,1152]{1,0:T(8,128)S(1)} %fusion.24, f32[128,1152]{1,0:T(8,128)S(1)} %fusion.25, f32[128,1152]{1,0:T(8,128)S(1)} %fusion.27, f32[128,1152]{1,0:T(8,128)S(1)} %fusion.14), kind=kOutput, calls=%fused_computation.7 | convolution fusion | flops 16314531840 | bytes 23003136 | tf_op jit(solution)/shard_map/dot_general | solution.py:17
  499.0 53.1 %reduce-scatter.2.cloned.1.call-done = f32[64,2304]{1,0:T(8,128)} async-done(((f32[512,2304]{1,0:T(8,128)}), f32[64,2304]{1,0:T(8,128)}) %reduce-scatter.2.cloned.1.call-update) | async-done | bytes 589840 | tf_op jit(solution)/shard_map/reduce_scatter | solution.py:27
  554.6 11.7 %psum.15 = f32[64]{0:T(128)S(1)} all-reduce(f32[64]{0:T(128)S(1)} %multiply_reduce_fusion), channel_id=1, replica_groups=mesh['wide'=8,'narrow'=4] {'narrow'}, use_global_device_ids=true, to_apply=%region_12.13 | all-reduce | flops 64 | bytes 512 | tf_op jit(solution)/shard_map/psum | solution.py:30
  566.4 12.1 %all-reduce.1 = f32[512]{0:T(512)S(1)} all-reduce(f32[512]{0:T(512)S(1)} %get-tuple-element.31), channel_id=1, replica_groups=mesh['wide'=8,'narrow'=4] {'wide'}, use_global_device_ids=true, to_apply=%add.1 | all-reduce | flops 512 | bytes 4096
  580.5 12.3 %all-gather.7.cloned.1.call-done = f32[512,2304]{1,0:T(8,128)} async-done(((f32[64,2304]{1,0:T(8,128)}), f32[512,2304]{1,0:T(8,128)}) %all-gather.7.cloned.1.call-update) | async-done | bytes 4718608 | tf_op jit(solution)/shard_map/all_gather | solution.py:34
  592.8 24.1 %fusion = f32[1152,2304]{1,0:T(8,128)} fusion(f32[512,2304]{1,0:T(8,128)} %all-gather.7.cloned.1.call-done, f32[1152,2304]{1,0:T(8,128)} %param.3, bf16[1152,2304]{1,0:T(8,128)(2,1)} %param.4, f32[128,1152]{1,0:T(8,128)S(1)} %fusion.24, f32[128,1152]{1,0:T(8,128)S(1)} %copy-done.1, f32[128,1152]{1,0:T(8,128)S(1)} %fusion.27, f32[128,1152]{1,0:T(8,128)S(1)} %fusion.14), kind=kOutput, calls=%fused_computation.3 | convolution fusion | flops 16319840256 | bytes 33619968 | tf_op jit(solution)/shard_map/dot_general | solution.py:17
  616.9 20.7 %convolution_convert_fusion = bf16[1152,2304]{1,0:T(8,128)(2,1)} fusion(f32[512,2304]{1,0:T(8,128)S(1)} %copy-done.2, f32[512]{0:T(512)S(1)} %all-reduce.1, f32[128,1152]{1,0:T(8,128)S(1)} %fusion.24, f32[128,1152]{1,0:T(8,128)S(1)} %copy-done.1, f32[128,1152]{1,0:T(8,128)S(1)} %fusion.27, f32[128,1152]{1,0:T(8,128)S(1)} %fusion.14), kind=kOutput, calls=%fused_computation.4 | convolution fusion | flops 16313057280 | bytes 12388352 | tf_op jit(solution)/shard_map/dot_general | solution.py:17
  (78 shorter events, 44.4 us)
Async XLA Ops:
  7.2 44.2 %all-gather.5.cloned.1.call-start = ((), (), s32[]{:S(2)}) async-start(), calls=%async_computation.1 | async-start | bytes 5308416 | tf_op jit(solution)/shard_map/all_gather | solution.py:22
  7.9 233.3 %all-gather.9.cloned.1.call-start = ((), (), s32[]{:S(2)}) async-start(), calls=%async_computation.5 | async-start | bytes 11796480 | tf_op jit(solution)/shard_map/all_gather | solution.py:23
  74.3 232.4 %all-reduce.4.cloned.1.call-start = ((), (), s32[]{:S(2)}) async-start(), calls=%async_computation.2 | async-start | bytes 2097152 | tf_op jit(solution)/shard_map/psum | solution.py:24
  251.7 300.5 %reduce-scatter.2.cloned.1.call-start = ((), (), s32[]{:S(2)}) async-start(), calls=%async_computation.3 | async-start | bytes 5308416 | tf_op jit(solution)/shard_map/reduce_scatter | solution.py:27
  306.7 2.6 copy-start.3
  310.8 1.0 copy-start.4
  336.0 0.7 copy-start.5
  462.2 0.8 copy-start.6
  462.2 13.6 %slice-start = ((s8[5308416]{0:T(1024)(128)(4,1)}), s8[4194304]{0:T(1024)(128)(4,1)S(1)}, s32[]{:S(2)}) async-start(s8[5308416]{0:T(1024)(128)(4,1)} %bitcast.59), calls=%async_computation.6 | async-start | bytes 8388608
  465.4 4.7 copy-start.7
  467.0 8.8 %slice-start.1 = ((s8[5308416]{0:T(1024)(128)(4,1)}), s8[1114112]{0:T(1024)(128)(4,1)S(1)}, s32[]{:S(2)}) async-start(s8[5308416]{0:T(1024)(128)(4,1)} %bitcast.59), calls=%async_computation.7 | async-start | bytes 2228224
  470.8 5.0 copy-start
  498.9 53.2 %copy-start.8 = (u32[32]{0:T(128)S(1)}, u32[32]{0:T(128)}, u32[]{:S(2)}) copy-start(u32[32]{0:T(128)} %constant.172) | copy-start | bytes 388
  499.0 93.8 %copy-start.1 = (f32[128,1152]{1,0:T(8,128)S(1)}, f32[128,1152]{1,0:T(8,128)}, u32[]{:S(2)}) copy-start(f32[128,1152]{1,0:T(8,128)} %copy-done) | copy-start | bytes 1769476
  499.0 93.8 %all-gather.7.cloned.1.call-start = ((), (), s32[]{:S(2)}) async-start(), calls=%async_computation.4 | async-start | bytes 5308416 | tf_op jit(solution)/shard_map/all_gather | solution.py:34
  592.8 24.1 %copy-start.2 = (f32[512,2304]{1,0:T(8,128)S(1)}, f32[512,2304]{1,0:T(8,128)}, u32[]{:S(2)}) copy-start(f32[512,2304]{1,0:T(8,128)} %all-gather.7.cloned.1.call-done) | copy-start | bytes 14155780
Sparse Core Ops, SparseCore 0:
  9.9 41.4 all-gather.4
  74.4 166.7 all-gather.8
  251.8 54.8 all-reduce.3
  499.1 53.0 reduce-scatter.1
  553.9 38.8 all-gather.6
